TPU v7x, 128 devices: a whole 4x4x4 slice. The times are simulated.
128 devices in a mesh: row: 16 (over y, x_hi, core), col: 8 (over x_lo, z).
Axes of the slice: x: 4 (x_hi: 2, x_lo: 2; x = x_hi * 2 + x_lo), y: 4, z: 4, core: 2. Of those that a mesh axis runs over, the one named last changes fastest.
Arguments:
- matrix: float32 [8, 16, 128, 16, 8, 128], P(None, 'row', None, None, 'col'), may hold values from -6 to 6
- reflectors: float32 [16, 8, 128, 512], P(None, 'col'), as said below
Outputs:
- updated: float32 [8, 16, 128, 16, 8, 128], P(None, 'row', None, None, 'col')
Inputs may be any that keep to these rules, and one draw needn't show every extreme that they name: Read as a 16384 x 512 matrix, the columns of reflectors are orthonormal.
All inputs are finite; a program needn't handle non-finite values.
Results may differ from a plain program's by a relative error of at most 0.0001.
Values sent between devices are 32-bit elements; how exact they have to be, the bound alone decides.
A program may use at most 128 MiB of HBM per device.

v0:
```python
import jax
import jax.numpy as jnp
from jax import lax
from jax.sharding import PartitionSpec as P


def from_root(value, axis, source):
    kept = jnp.where(lax.axis_index(axis) == source, value, 0).astype(value.dtype)
    return lax.psum(kept, axis)


def rows_for(lines, peers):
    spare = -len(lines) % peers
    return jnp.pad(lines, [(0, spare)] + [(0, 0)] * (lines.ndim - 1))


def sum_by_parts(x, axis):
    lines = x.reshape(-1, *x.shape[1:][-1:])
    own = lax.psum_scatter(
        rows_for(lines, lax.axis_size(axis)), axis, scatter_dimension=0, tiled=True
    )
    whole = lax.all_gather(own, axis).reshape(-1, *lines.shape[1:])
    return lax.slice_in_dim(whole, 0, len(lines)).reshape(x.shape)


def per_device(matrix, reflectors):
    row_count = lax.axis_size("row")
    col_count = lax.axis_size("col")
    stride = row_count // col_count
    row_index = lax.axis_index("row")
    col_index = lax.axis_index("col")
    row_tiles, _, tile_size, col_tiles, _, _ = matrix.shape
    total_rank = reflectors.shape[3]
    local_rows = row_tiles * tile_size
    local_cols = col_tiles * tile_size
    current = matrix.reshape(local_rows, local_cols)
    row_ids = (
        (jnp.arange(row_tiles)[:, None] * row_count + row_index) * tile_size
        + jnp.arange(tile_size)[None, :]
    ).reshape(-1)
    col_ids = (
        (jnp.arange(col_tiles)[:, None] * col_count + col_index) * tile_size
        + jnp.arange(tile_size)[None, :]
    ).reshape(-1)
    lower_mask = row_ids[:, None] >= col_ids[None, :]
    strict_mask = row_ids[:, None] > col_ids[None, :]
    refl_cols = reflectors.reshape(local_cols, total_rank)

    def pick_rows(source):
        breadth = source.shape[1]
        blocks = source.reshape(row_tiles, stride, tile_size, breadth)
        chosen = lax.dynamic_index_in_dim(blocks, row_index // col_count, axis=1, keepdims=False)
        return chosen.reshape(local_rows, breadth)

    def matmul(left_side, right_side):
        return jnp.dot(
            left_side,
            right_side,
            precision=lax.Precision.HIGHEST,
            preferred_element_type=jnp.float32,
        )

    def inner(left_side, right_side):
        return lax.dot_general(
            left_side,
            right_side,
            (((0,), (0,)), ((), ())),
            precision=lax.Precision.HIGHEST,
            preferred_element_type=jnp.float32,
        )

    refl_rows = from_root(pick_rows(refl_cols), "col", row_index % col_count)
    direct_part = matmul(jnp.where(lower_mask, current, 0.0), refl_cols)
    trans_part = inner(jnp.where(strict_mask, current, 0.0), refl_rows)
    direct = lax.psum(direct_part, "col")
    transposed = sum_by_parts(trans_part, "row")
    w_rows = direct + from_root(pick_rows(transposed), "col", row_index % col_count)
    breadth = direct.shape[1]
    pieces = []
    for offset in range(stride):
        moved = from_root(direct, "row", col_index + offset * col_count)
        pieces.append(moved.reshape(row_tiles, tile_size, breadth))
    w_cols = transposed + jnp.stack(pieces, axis=1).reshape(local_cols, breadth)
    projection = lax.psum(inner(refl_rows, w_rows), "row")
    w_rows = w_rows - 0.5 * matmul(refl_rows, projection)
    w_cols = w_cols - 0.5 * matmul(refl_cols, projection)
    left_side = jnp.concatenate([refl_rows, w_rows], axis=1)
    right_side = jnp.concatenate([w_cols, refl_cols], axis=1)
    current = current - lax.dot_general(
        left_side,
        right_side,
        (((1,), (1,)), ((), ())),
        precision=lax.Precision.HIGHEST,
        preferred_element_type=jnp.float32,
    )
    return jnp.where(lower_mask, current, 0.0).reshape(matrix.shape)


def solution(mesh):
    placed = (P(None, "row", None, None, "col", None), P(None, "col", None, None))
    return jax.shard_map(
        per_device,
        mesh=mesh,
        in_specs=placed,
        out_specs=P(None, "row", None, None, "col", None),
        check_vma=False,
    )
```

profile of v0, /device:TPU:3, one launch (start us, length us, event | category | flops | bytes accessed | tf_op | source)
XLA Modules:
  0.0 592.8 jit_solution(9861063768099171922)
XLA Ops:
  6.5 0.0 all-reduce.6.cloned.1.call-start
  6.5 3.2 bitcast_select_fusion.3
  9.8 0.0 all-reduce.6.cloned.1.call-update
  9.8 0.0 reduce-scatter.2.cloned.1.call-start
  9.9 0.1 iota_add_fusion.1
  9.9 0.1 iota_add_fusion
  10.0 80.2 %all-reduce.6.cloned.1.call-done = f32[1024,512]{1,0:T(8,128)} async-done(((f32[1024,512]{1,0:T(8,128)}), f32[1024,512]{1,0:T(8,128)}) %all-reduce.6.cloned.1.call-update) | async-done | bytes 2097168 | tf_op jit(solution)/shard_map/psum | solution.py:9
  90.2 19.5 %fusion.4 = f32[2048,512]{1,0:T(8,128)} fusion(f32[1024,512]{1,0:T(8,128)} %all-reduce.6.cloned.1.call-done, f32[128,8,16,128]{3,2,1,0:T(8,128)} %bitcast.60, s32[2048]{0:T(1024)S(1)} %get-tuple-element.16, s32[1024]{0:T(1024)S(1)} %get-tuple-element.14), kind=kOutput, calls=%fused_computation.7 | convolution fusion | flops 12889096192 | bytes 14692352 | tf_op jit(solution)/shard_map/dot_general | solution.py:64
  109.7 0.0 reduce-scatter.2.cloned.1.call-update
  109.8 0.0 all-gather.3.cloned.1.call-start
  109.8 83.1 %reduce-scatter.2.cloned.1.call-done = f32[128,512]{1,0:T(8,128)} async-done(((f32[2048,512]{1,0:T(8,128)}), f32[128,512]{1,0:T(8,128)}) %reduce-scatter.2.cloned.1.call-update) | async-done | bytes 262160 | tf_op jit(solution)/shard_map/reduce_scatter | solution.py:19
  192.9 0.0 all-gather.3.cloned.1.call-update
  193.0 0.2 all-reduce.10.cloned.1.call-start
  193.2 0.0 copy-start
  193.2 32.2 %fusion = f32[8,128,16,128]{3,2,1,0:T(8,128)} fusion(f32[8,1,128,16,1,128]{5,4,3,2,1,0:T(1,128)} %param.2, s32[16,128]{1,0:T(8,128)S(1)} %get-tuple-element.15, s32[8,128]{1,0:T(8,128)S(1)} %get-tuple-element.13), kind=kLoop, calls=%fused_computation.1 | loop fusion | flops 4194304 | bytes 16789504 | tf_op jit(solution)/shard_map/jit(_where)/select_n | solution.py:73
  225.4 0.0 copy-done
  225.4 19.5 %fusion.1 = f32[1024,512]{1,0:T(8,128)} fusion(f32[2048,512]{1,0:T(8,128)S(1)} %bitcast.54, f32[128,8,16,128]{3,2,1,0:T(8,128)} %bitcast.64), kind=kOutput, calls=%fused_computation.2 | convolution fusion | flops 12884901888 | bytes 14680064 | tf_op jit(solution)/shard_map/dot_general | solution.py:56
  244.9 5.9 %all-gather.3.cloned.1.call-done = f32[2048,512]{1,0:T(8,128)} async-done(((f32[128,512]{1,0:T(8,128)}), f32[2048,512]{1,0:T(8,128)}) %all-gather.3.cloned.1.call-update) | async-done | bytes 4194320 | tf_op jit(solution)/shard_map/all_gather | solution.py:22
  250.9 3.2 bitcast_select_fusion.2
  254.1 0.0 all-reduce.10.cloned.1.call-update
  254.1 0.4 all-reduce.8.cloned.1.call-start
  254.6 102.6 %all-reduce.10.cloned.1.call-done = (f32[1024,512]{1,0:T(8,128)}, f32[1024,512]{1,0:T(8,128)}) async-done(((f32[1024,512]{1,0:T(8,128)}, f32[1024,512]{1,0:T(8,128)}), (f32[1024,512]{1,0:T(8,128)}, f32[1024,512]{1,0:T(8,128)})) %all-reduce.10.cloned.1.call-update) | async-done | bytes 4194320 | tf_op jit(solution)/shard_map/psum | solution.py:75
  357.2 0.0 copy-start.3
  357.2 5.4 fusion.27
  362.6 0.0 copy-done.3
  362.6 4.6 fusion.28
  367.2 0.0 all-reduce.8.cloned.1.call-update
  367.2 159.5 %all-reduce.8.cloned.1.call-done = (f32[8,1,128,512]{3,2,0,1:T(8,128)}, f32[8,1,128,512]{3,2,0,1:T(8,128)}, f32[512,512]{1,0:T(8,128)}) async-done(((f32[8,1,128,512]{3,2,0,1:T(8,128)}, f32[8,1,128,512]{3,2,0,1:T(8,128)}, f32[512,512]{1,0:T(8,128)}), (f32[8,1,128,512]{3,2,0,1:T(8,128)}, f32[8,1,128,512]{3,2,0,1:T(8,128)}, f32[512,512]{1,0:T(8,128)})) %all-reduce.8.cloned.1.call-update) | async-done | bytes 5242896 | tf_op jit(solution)/shard_map/psum | solution.py:9
  526.8 2.7 pad_maximum_fusion
  529.5 0.0 copy-start.4
  529.5 0.0 copy-start.5
  529.5 0.0 copy-start.2
  529.5 0.6 copy.5
  530.1 0.0 copy-start.1
  530.1 0.9 copy-done.4
  531.1 0.3 copy-done.5
  531.3 0.0 slice-start
  531.3 4.8 multiply_subtract_fusion
  536.1 0.0 copy-done.2
  536.1 0.0 copy-done.1
  536.1 0.0 slice-start.1
  536.1 0.0 copy-start.6
  536.1 7.5 %bitcast_subtract_fusion.1 = f32[2048,512]{1,0:T(8,128)S(1)} fusion(f32[2048,512]{1,0:T(8,128)S(1)} %copy-done.2, f32[8,2,128,512]{3,2,1,0:T(8,128)S(1)} %copy.5, f32[512,512]{1,0:T(8,128)S(1)} %copy-done.5, f32[2048,512]{1,0:T(8,128)S(1)} %bitcast.55), kind=kOutput, calls=%fused_computation.20 | convolution fusion | flops 6445596672 | bytes 17825792 | tf_op jit(solution)/shard_map/dot_general | solution.py:56
  543.7 0.0 slice-done
  543.7 0.0 slice-done.1
  543.7 0.0 copy-done.6
  543.7 33.6 %fusion.6 = f32[128,8,16,128]{3,1,2,0:T(8,128)} fusion(f32[128,8,16,128]{3,2,1,0:T(8,128)S(1)} %bitcast.63, s32[2048]{0:T(1024)S(1)} %get-tuple-element.16, s32[1024]{0:T(1024)S(1)} %get-tuple-element.14, f32[2048,512]{1,0:T(8,128)S(1)} %bitcast.56, f32[2048,512]{1,0:T(8,128)S(1)} %bitcast_subtract_fusion.1, f32[1024,512]{1,0:T(8,128)S(1)} %copy-done.6, ...), kind=kOutput, calls=%fused_computation.9 | convolution fusion | flops 25779240960 | bytes 29372416 | tf_op jit(solution)/shard_map/dot_general | solution.py:89
  577.3 8.8 %copy.11 = f32[128,8,16,128]{3,2,1,0:T(8,128)} copy(f32[128,8,16,128]{3,1,2,0:T(8,128)} %fusion.6) | data formatting | bytes 16777216
  (3 shorter events, 0.0 us)
Async XLA Ops:
  6.5 83.6 %all-reduce.6.cloned.1.call-start = ((), (), s32[]{:S(2)}) async-start(), calls=%async_computation.1 | async-start | bytes 4194304 | tf_op jit(solution)/shard_map/psum | solution.py:9
  9.8 183.2 %reduce-scatter.2.cloned.1.call-start = ((), (), s32[]{:S(2)}) async-start(), calls=%async_computation.2 | async-start | bytes 4456448 | tf_op jit(solution)/shard_map/reduce_scatter | solution.py:19
  109.8 141.1 %all-gather.3.cloned.1.call-start = ((), (), s32[]{:S(2)}) async-start(), calls=%async_computation.3 | async-start | bytes 4456448 | tf_op jit(solution)/shard_map/all_gather | solution.py:22
  193.0 164.2 %all-reduce.10.cloned.1.call-start = ((), (), s32[]{:S(2)}) async-start(), calls=%async_computation.5 | async-start | bytes 8388608 | tf_op jit(solution)/shard_map/psum | solution.py:75
  193.2 32.2 %copy-start = (f32[16,1,128,512]{3,2,1,0:T(8,128)S(1)}, f32[16,1,128,512]{3,2,1,0:T(8,128)}, u32[]{:S(2)}) copy-start(f32[16,1,128,512]{3,2,1,0:T(8,128)} %param.3) | copy-start | bytes 12582916
  254.1 272.7 %all-reduce.8.cloned.1.call-start = ((), (), s32[]{:S(2)}) async-start(), calls=%async_computation.4 | async-start | bytes 10485760 | tf_op jit(solution)/shard_map/psum | solution.py:9
  357.2 5.4 copy-start.3
  529.5 1.6 copy-start.4
  529.5 1.8 copy-start.5
  529.5 6.6 %copy-start.2 = (f32[2048,512]{1,0:T(8,128)S(1)}, f32[2048,512]{1,0:T(8,128)}, u32[]{:S(2)}) copy-start(f32[2048,512]{1,0:T(8,128)} %all-gather.3.cloned.1.call-done) | copy-start | bytes 12582916
  530.1 6.0 %copy-start.1 = (f32[16,1,128,512]{3,2,1,0:T(8,128)S(1)}, f32[16,1,128,512]{3,2,1,0:T(8,128)}, u32[]{:S(2)}) copy-start(f32[16,1,128,512]{3,2,1,0:T(8,128)} %param.3) | copy-start | bytes 12582916
  531.3 12.3 %slice-start = ((s8[8388608]{0:T(1024)(128)(4,1)}), s8[4194304]{0:T(1024)(128)(4,1)S(1)}, s32[]{:S(2)}) async-start(s8[8388608]{0:T(1024)(128)(4,1)} %bitcast.61), calls=%async_computation.6 | async-start | bytes 8388608
  536.1 7.6 %slice-start.1 = ((s8[8388608]{0:T(1024)(128)(4,1)}), s8[4194304]{0:T(1024)(128)(4,1)S(1)}, s32[]{:S(2)}) async-start(s8[8388608]{0:T(1024)(128)(4,1)} %bitcast.61), calls=%async_computation.7 | async-start | bytes 8388608
  536.1 7.6 %copy-start.6 = (f32[1024,512]{1,0:T(8,128)S(1)}, f32[1024,512]{1,0:T(8,128)}, u32[]{:S(2)}) copy-start(f32[1024,512]{1,0:T(8,128)} %multiply_subtract_fusion) | copy-start | bytes 6291460
Sparse Core Ops, SparseCore 0:
  9.9 80.2 all-reduce.5
  109.9 83.0 reduce-scatter.1
  195.4 55.4 all-gather.2
  254.2 102.8 all-reduce.9
  367.3 159.3 all-reduce.7
where the time goes:
time: 602 us; the launch traced here: 593 us
  waiting for transfers between devices  431 us (72%)
  matrix products  89.6 us (15%)
  other arithmetic  46.9 us (8%)
  between operations  13.5 us (2%)
  local copies, waits for them, and re-layouts  10.6 us (2%)
    psum x2, waiting for transfers between devices, from_root(): return lax.psum(kept, axis)  240 us
    psum x1, waiting for transfers between devices, per_device(): direct = lax.psum(direct_part, 'col')  103 us
    reduce_scatter x1, waiting for transfers between devices, sum_by_parts(): lax.psum_scatter(rows_for(lines, lax.axis_size(axis)), axis, scatter_dime...  83.1 us
    dot_general x1, matrix products, per_device(): lax.dot_general(left_side, right_side, (((1,), (1,)), ((), ())), precisio...  33.6 us
    select_n x1, other arithmetic, per_device(): direct_part = matmul(jnp.where(lower_mask, current, 0.0), refl_cols)  32.2 us
    dot_general x3, matrix products, matmul(): jnp.dot(left_side, right_side, precision=lax.Precision.HIGHEST, preferred...  31.8 us
    dot_general x2, matrix products, inner(): lax.dot_general(left_side, right_side, (((0,), (0,)), ((), ())), precisio...  24.1 us
  transfers between devices with their start and end apart: 5, of which 5 were waited for; matrix products, arithmetic and copies ran while one was open for 9% of the time, Pallas kernels for 0%

commit v1 on v0

v1 whole, which is shorter than its diff:
```python
import jax
import jax.numpy as jnp
from jax import lax
from jax.experimental import pallas as pl
from jax.experimental.pallas import tpu as pltpu
from jax.sharding import PartitionSpec as P

MESH = pl.DeviceIdType.MESH
F32 = jnp.float32
BF16 = jnp.bfloat16
NC = 4
PLAN = (
    ("prep", (2, 0, 3)), ("dc", (3,)), ("v1", (0,)), ("dc", (2,)), ("v1", (1,)), ("prep", (1,)), ("v1", (2,)),
    ("v2", (0,)), ("dc", (1, 0)), ("d1", (3,)), ("v2", (1,)), ("v1", (3,)), ("d1", (0,)), ("v3", (0, 1)),
    ("v2", (2,)), ("vt", (0,)), ("d1", (1,)), ("v2", (3,)), ("vt", (1,)), ("v3", (2,)), ("t2", (0,)), ("v3", (3,)),
    ("t2", (1,)), ("dx", (0,)), ("vt", (2,)), ("d1", (2,)), ("dx", (3, 1)), ("t3", (1, 0)), ("vt", (3,)),
    ("t2", (2,)), ("t4", (1,)), ("d2", (1,)), ("t4", (0,)), ("d2", (0,)), ("dx", (2,)), ("t3", (2,)), ("d3", (1,)),
    ("t5", (1,)), ("t2", (3,)), ("d3", (0,)), ("rz", (1,)), ("t4", (2,)), ("d2", (2,)), ("t5", (0,)), ("t3", (3,)),
    ("cx", (1,)), ("t5", (2,)), ("rz", (0,)), ("d2", (3,)), ("d3", (2,)), ("t4", (3,)), ("a2", (1,)), ("rz", (2,)),
    ("cx", (0,)), ("d3", (3,)), ("t5", (3,)), ("cx", (2,)), ("a3", (1,)), ("rz", (3,)), ("a2", (0,)), ("cx", (3,)),
    ("a2", (2,)), ("a3", (0,)), ("a2", (3,)), ("a3", (2,)), ("a4", (0, 1)), ("a3", (3,)), ("a4", (2,)), ("a5", (0,)),
    ("a4", (3,)), ("a5", (2, 1, 3)),
)
RANK = 512
W = RANK // NC
Q = W // 4
UW = W + Q

RINGS = ("V", "A", "B", "D", "T")
OPS = [a + b for a in RINGS for b in ("1", "2p", "2m", "3p", "3m", "4", "5p", "5m")]
OPS += ["V0", "CD", "CT"] + ["R1", "R2", "R3", "R4"]
OP = {name: n for n, name in enumerate(OPS)}


def split(x):
    hi = x.astype(BF16)
    return hi, (x - hi.astype(F32)).astype(BF16)


def dot(a, b):
    return jnp.dot(a, b, preferred_element_type=F32)


def dot_nt(a, b):
    return lax.dot_general(a, b, (((1,), (1,)), ((), ())), preferred_element_type=F32)


def block(i, j):
    return i * (i + 1) // 2 + j


def xor(a, b):
    return a + b - 2 * a * b


def exchange(
    mat, refl, out,
    sbuf, sh, sl, vc, vcs, vr, vrs, vrt, dbuf, dh, dl, dr, d2r,
    ubuf, t1r, t2r, t3r, crd, crt, rx, gbuf, wr, mm, wcts, wrs, zero,
    ssem, rsem, msem, vsem, osem,
):
    r, c = lax.axis_index("row"), lax.axis_index("col")
    div, rem = lax.div, lax.rem
    core, y = rem(r, 2), div(r, 4)
    xh = rem(div(r, 2), 2)
    z, xl = rem(c, 4), div(c, 4)
    half, low = div(r, 8), rem(r, 8)
    alone = low == c
    y0, z1, z0 = rem(y, 2), div(z, 2), rem(z, 2)
    yp, ym, y2 = rem(y + 1, 4), rem(y + 3, 4), rem(y + 2, 4)
    zp, zm, z2 = rem(z + 1, 4), rem(z + 3, 4), rem(z + 2, 4)
    to_core = {"row": r + 1 - 2 * core}
    to_xh = {"row": r + 2 - 4 * xh}
    to_yp, to_ym = {"row": yp * 4 + rem(r, 4)}, {"row": ym * 4 + rem(r, 4)}
    to_xl = {"col": c + 4 - 8 * xl}
    to_zp, to_zm = {"col": xl * 4 + zp}, {"col": xl * 4 + zm}
    flip = xor(z1, xl)
    to_t = {"row": half * 8 + 4 * xor(xor(z1, xh), y0) + 2 * xor(xor(xl, y0), xh) + z0, "col": low}
    dxl, dz1 = xor(xh, flip), xor(y0, flip)
    to_d = {"row": half * 8 + c, "col": dxl * 4 + dz1 * 2 + core}
    dz = dz1 * 2 + core
    own = 2 * (4 * xor(xh, z1) + 2 * dz1 + core) + half

    def row_slot(k):
        return k % 4, 1 - y0 if k // 4 else y0

    def col_slot(m):
        k, h = m // 2, m % 2
        return k % 2, 2 * h + (1 - flip if (k // 2) % 2 else flip), 1 - z1 if k // 4 else z1

    barrier = pltpu.get_barrier_semaphore()
    peers = [to_core, to_xh, to_yp, to_ym] + [to_xl] + [{"col": xl * 4 + rem(z + d, 4)} for d in range(1, 4)]
    for dev in peers:
        pl.semaphore_signal(barrier, inc=1, device_id=dev, device_id_type=MESH)

    @pl.when(jnp.logical_not(alone))
    def _():
        pl.semaphore_signal(barrier, inc=1, device_id=to_t, device_id_type=MESH)
        pl.semaphore_signal(barrier, inc=1, device_id=to_d, device_id_type=MESH)

    def local_vc():
        return pltpu.make_async_copy(refl, vc, vsem)

    local_vc().start()

    def s_copy(i, kk, m):
        return pltpu.make_async_copy(
            mat.at[2 * i + kk, 0, :, m, 0, :],
            sbuf.at[2 * i * (i + 1) + m, pl.ds(kk * 128, 128)],
            msem.at[2 * i + kk, m],
        )

    for i in range(4):
        @pl.loop(0, 4 * (i + 1))
        def _(m):
            s_copy(i, 0, m).start()
            s_copy(i, 1, m).start()

    local_vc().wait()
    for i in range(8):
        rows = pl.ds(i * 256, 256)
        vcs[0, rows, :], vcs[1, rows, :] = split(vc[rows, :])
    zero[...] = jnp.zeros_like(zero)

    def z_copy(i, kk, m):
        return pltpu.make_async_copy(zero, out.at[2 * i + kk, 0, :, m, 0, :], osem.at[2 * i + kk, m])

    def o_copy(i, kk, m):
        return pltpu.make_async_copy(
            sbuf.at[2 * i * (i + 1) + m, pl.ds(kk * 128, 128)],
            out.at[2 * i + kk, 0, :, m, 0, :],
            osem.at[2 * i + kk, m],
        )

    @pl.when(alone)
    def _():
        pl.semaphore_wait(barrier, len(peers))

    @pl.when(jnp.logical_not(alone))
    def _():
        pl.semaphore_wait(barrier, len(peers) + 2)

    def send(op, j, src, dst, dev):
        return pltpu.make_async_remote_copy(
            src_ref=src, dst_ref=dst, send_sem=ssem.at[j, OP[op]], recv_sem=rsem.at[j, OP[op]],
            device_id=dev, device_id_type=MESH,
        )

    sent = []

    def start(op, j, src, dst, dev):
        copy = send(op, j, src, dst, dev)
        copy.start()
        sent.append(copy)

    def got(op, j, dst):
        send(op, j, dst, dst, to_core).wait_recv()

    def v_copy(j):
        return send(
            "V0", j, refl.at[pl.ds(pl.multiple_of(own * 128, 128), 128), pl.ds(j * W, W)],
            vr.at[j, dz, dxl], to_d,
        )

    @pl.when(jnp.logical_not(alone))
    def _():
        for j in range(NC):
            v_copy(j).start()

    def diagonal(i):
        ia = lax.broadcasted_iota(jnp.int32, (256, 128), 0)
        ib = lax.broadcasted_iota(jnp.int32, (256, 128), 1)
        return (i * 2 + lax.shift_right_logical(ia, 7)) * 2048 + r * 128 + (ia & 127) - ib - c * 128

    def prep(i):
        line = diagonal(i)

        for m in range(4 * (i + 1)):
            s_copy(i, 0, m).wait()
            s_copy(i, 1, m).wait()
            x = sbuf[2 * i * (i + 1) + m]
            if m // 4 == i:
                gap = line - m * 1024
                x = jnp.where(gap > 0, x, jnp.where(gap == 0, 0.5 * x, 0.0))
            b = block(i, m // 4)
            cols = pl.ds((m % 4) * 128, 128)
            sh[b, :, cols], sl[b, :, cols] = split(x)

        @pl.loop(4 * (i + 1), 16)
        def _(m):
            z_copy(i, 0, m).start()
            z_copy(i, 1, m).start()

    def d_compute(i):
        acc = None
        for j in range(i + 1):
            b = block(i, j)
            rows = pl.ds(j * 512, 512)
            part = (
                dot(sh[b], vcs[0, rows, :]) + dot(sh[b], vcs[1, rows, :]) + dot(sl[b], vcs[0, rows, :])
            )
            acc = part if acc is None else acc + part
        rows = pl.ds(i * 256, 256)
        dh[rows, :], dl[rows, :] = split(acc)
        for kk in range(2):
            k = 2 * i + kk
            for j in range(NC):
                zk, xk = row_slot(k)
                dbuf[j, xk, zk] = acc[kk * 128:(kk + 1) * 128, j * W:(j + 1) * W]

    def v1(j):
        @pl.when(jnp.logical_not(alone))
        def _():
            got("V0", j, vr.at[j, z, xl])

        @pl.when(alone)
        def _():
            vr[j, z, xl] = vc[pl.ds(pl.multiple_of(own * 128, 128), 128), pl.ds(j * W, W)]

        start("V1", j, vr.at[j, z, xl], vr.at[j, z, xl], to_xl)

    def v2(j):
        got("V1", j, vr.at[j, z, 1 - xl])
        start("V2p", j, vr.at[j, z], vr.at[j, z], to_zp)
        start("V2m", j, vr.at[j, z], vr.at[j, z], to_zm)

    def v3(j):
        got("V2p", j, vr.at[j, zm])
        start("V3p", j, vr.at[j, zm, 0], vr.at[j, zm, 0], to_zp)
        got("V2m", j, vr.at[j, zp])
        start("V3m", j, vr.at[j, zp, 1], vr.at[j, zp, 1], to_zm)

    def v4(j):
        got("V3p", j, vr.at[j, z2, 0])
        got("V3m", j, vr.at[j, z2, 1])

    def t_compute(j):
        for k in range(8):
            zk, xk = row_slot(k)
            x = vr[j, zk, xk]
            i, kk = k // 2, k % 2
            rows, cols = pl.ds(kk * 128, 128), pl.ds(j * W, W)
            vrs[i, 0, rows, cols], vrs[i, 1, rows, cols] = split(x)
            xt = x.T
            cols = pl.ds(k * 128, 128)
            vrt[0:W, cols], vrt[W:2 * W, cols] = split(xt)
        for jj in range(4):
            acc = None
            for i in range(jj, 4):
                b = block(i, jj)
                cols = pl.ds(i * 256, 256)
                both = dot(vrt[:, cols], sh[b])
                part = both[:W] + both[W:] + dot(vrt[0:W, cols], sl[b])
                acc = part if acc is None else acc + part
            for mi in range(4):
                k0, yy, k1 = col_slot(4 * jj + mi)
                ubuf[j, k0, yy, k1, 0:W, :] = acc[:, mi * 128:(mi + 1) * 128]
        both = dot(vrt[...], dh[...])
        acc = both[:W] + both[W:] + dot(vrt[0:W, :], dl[...])
        for m in range(16):
            q = m % 4
            ubuf[j, m // 8, (m // 2) % 4, m % 2, W:UW, :] = (
                acc[q * Q:(q + 1) * Q, (m // 4) * 128:(m // 4 + 1) * 128]
            )

    first, second = pl.ds(0, 64), pl.ds(64, 64)

    def d1(j):
        start("D1", j, dbuf.at[j, 1 - xl], d2r.at[j], to_xl)

    def dx(j):
        got("D1", j, d2r.at[j])
        dbuf[j, xl, z2] = dbuf[j, xl, z2] + d2r[j, z2]
        start("D2p", j, dbuf.at[j, xl, z2, first], dr.at[j, 0], to_zp)
        start("D2m", j, dbuf.at[j, xl, z2, second], dr.at[j, 2], to_zm)
        dbuf[j, xl, zp] = dbuf[j, xl, zp] + d2r[j, zp]
        dbuf[j, xl, zm] = dbuf[j, xl, zm] + d2r[j, zm]
        start("D3p", j, dbuf.at[j, xl, zp, second], dr.at[j, 1], to_zp)
        start("D3m", j, dbuf.at[j, xl, zm, first], dr.at[j, 3], to_zm)
        dbuf[j, xl, z] = dbuf[j, xl, z] + d2r[j, z]

    def d2(j):
        got("D2p", j, dr.at[j, 0])
        dbuf[j, xl, zp, first] = dbuf[j, xl, zp, first] + dr[j, 0]
        start("D5p", j, dbuf.at[j, xl, zp, first], dr.at[j, 4], to_zp)
        got("D2m", j, dr.at[j, 2])
        dbuf[j, xl, zm, second] = dbuf[j, xl, zm, second] + dr[j, 2]
        start("D5m", j, dbuf.at[j, xl, zm, second], dr.at[j, 5], to_zm)

    def d3(j):
        got("D3p", j, dr.at[j, 1])
        got("D3m", j, dr.at[j, 3])
        got("D5p", j, dr.at[j, 4])
        dbuf[j, xl, z, first] = dbuf[j, xl, z, first] + dr[j, 3] + dr[j, 4]
        got("D5m", j, dr.at[j, 5])
        dbuf[j, xl, z, second] = dbuf[j, xl, z, second] + dr[j, 1] + dr[j, 5]

        @pl.when(jnp.logical_not(alone))
        def _():
            send("CD", j, dbuf.at[j, xl, z], crd.at[j], to_t).start()

    def t1(j):
        start("T1", j, ubuf.at[j, 1 - core], t1r.at[j], to_core)

    def t2(j):
        got("T1", j, t1r.at[j])
        ubuf[j, core, y2] = ubuf[j, core, y2] + t1r[j, y2]
        start("T2p", j, ubuf.at[j, core, y2, 0], t2r.at[j, 0], to_yp)
        start("T2m", j, ubuf.at[j, core, y2, 1], t2r.at[j, 2], to_ym)
        ubuf[j, core, yp] = ubuf[j, core, yp] + t1r[j, yp]
        ubuf[j, core, ym] = ubuf[j, core, ym] + t1r[j, ym]
        start("T3p", j, ubuf.at[j, core, yp, 1], t2r.at[j, 1], to_yp)
        start("T3m", j, ubuf.at[j, core, ym, 0], t2r.at[j, 3], to_ym)
        ubuf[j, core, y] = ubuf[j, core, y] + t1r[j, y]

    def t3(j):
        got("T2p", j, t2r.at[j, 0])
        ubuf[j, core, yp, 0] = ubuf[j, core, yp, 0] + t2r[j, 0]
        start("T5p", j, ubuf.at[j, core, yp, 0], t2r.at[j, 4], to_yp)
        got("T2m", j, t2r.at[j, 2])
        ubuf[j, core, ym, 1] = ubuf[j, core, ym, 1] + t2r[j, 2]
        start("T5m", j, ubuf.at[j, core, ym, 1], t2r.at[j, 5], to_ym)

    def t4(j):
        got("T3p", j, t2r.at[j, 1])
        got("T3m", j, t2r.at[j, 3])
        got("T5p", j, t2r.at[j, 4])
        ubuf[j, core, y, 0] = ubuf[j, core, y, 0] + t2r[j, 3] + t2r[j, 4]
        got("T5m", j, t2r.at[j, 5])
        ubuf[j, core, y, 1] = ubuf[j, core, y, 1] + t2r[j, 1] + t2r[j, 5]
        start("T4", j, ubuf.at[j, core, y, 1 - xh], t3r.at[j], to_xh)

    def t5(j):
        got("T4", j, t3r.at[j])
        ubuf[j, core, y, xh] = ubuf[j, core, y, xh] + t3r[j]

        @pl.when(jnp.logical_not(alone))
        def _():
            send("CT", j, ubuf.at[j, core, y, xh, 0:W], crt.at[j], to_d).start()

        start("R1", j, ubuf.at[j, core, y, xh, W:UW], rx.at[j, 0], to_xl)

    def rz(j):
        got("R1", j, rx.at[j, 0])
        rx[j, 1] = ubuf[j, core, y, xh, W:UW, :] + rx[j, 0]
        for d in range(1, 4):
            start(f"R{d + 1}", j, rx.at[j, 1], rx.at[j, 1 + d], {"col": xl * 4 + rem(z + d, 4)})

    def join(j):
        @pl.when(jnp.logical_not(alone))
        def _():
            got("CD", j, crd.at[j])
            got("CT", j, crt.at[j])

        @pl.when(alone)
        def _():
            crd[j] = dbuf[j, xl, z]
            crt[j] = ubuf[j, core, y, xh, 0:W, :]

        wr[j, z, xl] = dbuf[j, xl, z] + crt[j].T
        start("B1", j, wr.at[j, z, xl], wr.at[j, z, xl], to_xl)
        gbuf[j, core, y, xh, 0:W, :] = ubuf[j, core, y, xh, 0:W, :] + crd[j].T
        total = rx[j, 1]
        for d in range(1, 4):
            got(f"R{d + 1}", j, rx.at[j, 1 + d])
            total = total + rx[j, 1 + d]
        gbuf[j, core, y, xh, W:UW, :] = total
        start("A1", j, gbuf.at[j, core, y, xh], gbuf.at[j, core, y, xh], to_xh)

    def a2(j):
        got("B1", j, wr.at[j, z, 1 - xl])
        start("B2p", j, wr.at[j, z], wr.at[j, z], to_zp)
        start("B2m", j, wr.at[j, z], wr.at[j, z], to_zm)
        got("A1", j, gbuf.at[j, core, y, 1 - xh])
        start("A2p", j, gbuf.at[j, core, y], gbuf.at[j, core, y], to_yp)
        start("A2m", j, gbuf.at[j, core, y], gbuf.at[j, core, y], to_ym)

    def a3(j):
        got("B2p", j, wr.at[j, zm])
        start("B3p", j, wr.at[j, zm, 0], wr.at[j, zm, 0], to_zp)
        got("B2m", j, wr.at[j, zp])
        start("B3m", j, wr.at[j, zp, 1], wr.at[j, zp, 1], to_zm)
        got("A2p", j, gbuf.at[j, core, ym])
        start("A3p", j, gbuf.at[j, core, ym, 0], gbuf.at[j, core, ym, 0], to_yp)
        got("A2m", j, gbuf.at[j, core, yp])
        start("A3m", j, gbuf.at[j, core, yp, 1], gbuf.at[j, core, yp, 1], to_ym)

    def a4(j):
        got("A3p", j, gbuf.at[j, core, y2, 0])
        got("A3m", j, gbuf.at[j, core, y2, 1])
        start("A4", j, gbuf.at[j, core], gbuf.at[j, core], to_core)
        got("B3p", j, wr.at[j, z2, 0])
        got("B3m", j, wr.at[j, z2, 1])

    def a5(j):
        got("A4", j, gbuf.at[j, 1 - core])
        for m in range(16):
            k0, yy, k1 = col_slot(m)
            rows, cols = pl.ds(j * W, W), pl.ds(m * 128, 128)
            wcts[0, rows, cols], wcts[1, rows, cols] = split(gbuf[j, k0, yy, k1, 0:W, :])
            q = m % 4
            mm[pl.ds(j * W + q * Q, Q), pl.ds((m // 4) * 128, 128)] = (
                gbuf[j, m // 8, (m // 2) % 4, m % 2, W:UW, :]
            )

    def v_ready(j):
        v4(j)
        t_compute(j)
        t1(j)

    stages = {
        "prep": prep, "dc": d_compute, "v1": v1, "v2": v2, "v3": v3, "vt": v_ready,
        "d1": d1, "dx": dx, "d2": d2, "d3": d3, "t2": t2, "t3": t3, "t4": t4, "t5": t5, "rz": rz,
        "cx": join, "a2": a2, "a3": a3, "a4": a4, "a5": a5,
    }
    for name, order in PLAN:
        for n in order:
            stages[name](n)

    m_sum = mm[...] + mm[...].T
    mh, ml = split(m_sum)
    for i in range(4):
        both = dot(vrs[i].reshape(RANK, RANK), mh)
        fix = both[:256] + both[256:] + dot(vrs[i, 0], ml)
        for kk in range(2):
            k = 2 * i + kk
            for j in range(NC):
                zk, xk = row_slot(k)
                x = wr[j, zk, xk] - fix[kk * 128:(kk + 1) * 128, j * W:(j + 1) * W]
                rows, cols = pl.ds(kk * 128, 128), pl.ds(j * W, W)
                wrs[i, 0, rows, cols], wrs[i, 1, rows, cols] = split(x)
        for j in range(i + 1):
            part = pl.ds(j * 512, 512)
            both = dot(vrs[i].reshape(512, RANK), wcts[0, :, part])
            both = both + dot_nt(wrs[i].reshape(512, RANK), vcs[0, part, :])
            delta = (
                both[:256] + both[256:] + dot(vrs[i, 0], wcts[1, :, part]) + dot_nt(wrs[i, 0], vcs[1, part, :])
            )
            for mi in range(4):
                m = 4 * j + mi
                x = sbuf[2 * i * (i + 1) + m] - delta[:, mi * 128:(mi + 1) * 128]
                if i == j:
                    x = jnp.where(diagonal(i) >= m * 1024, x, 0.0)
                sbuf[2 * i * (i + 1) + m] = x
                for kk in range(2):
                    o_copy(i, kk, m).start()
    for copy in sent:
        copy.wait_send()

    @pl.when(jnp.logical_not(alone))
    def _():
        for j in range(NC):
            v_copy(j).wait_send()
            send("CD", j, dbuf.at[j, xl, z], crd.at[j], to_t).wait_send()
            send("CT", j, ubuf.at[j, core, y, xh, 0:W], crt.at[j], to_d).wait_send()

    for i in range(4):
        @pl.loop(0, 4 * (i + 1))
        def _(m):
            o_copy(i, 0, m).wait()
            o_copy(i, 1, m).wait()

        @pl.loop(4 * (i + 1), 16)
        def _(m):
            z_copy(i, 0, m).wait()
            z_copy(i, 1, m).wait()


def project(mat, refl):
    vm = pltpu.VMEM
    scratch = [
        vm((40, 256, 128), F32),
        vm((10, 256, 512), BF16),
        vm((10, 256, 512), BF16),
        vm((2048, RANK), F32),
        vm((2, 2048, RANK), BF16),
        vm((NC, 4, 2, 128, W), F32),
        vm((4, 2, 256, RANK), BF16),
        vm((2 * W, 1024), BF16),
        vm((NC, 2, 4, 128, W), F32),
        vm((1024, RANK), BF16),
        vm((1024, RANK), BF16),
        vm((NC, 6, 64, W), F32),
        vm((NC, 4, 128, W), F32),
        vm((NC, 2, 4, 2, UW, 128), F32),
        vm((NC, 4, 2, UW, 128), F32),
        vm((NC, 6, UW, 128), F32),
        vm((NC, UW, 128), F32),
        vm((NC, 128, W), F32),
        vm((NC, W, 128), F32),
        vm((NC, 5, Q, 128), F32),
        vm((NC, 2, 4, 2, UW, 128), F32),
        vm((NC, 4, 2, 128, W), F32),
        vm((RANK, RANK), F32),
        vm((2, RANK, 2048), BF16),
        vm((4, 2, 256, RANK), BF16),
        vm((128, 128), F32),
        pltpu.SemaphoreType.DMA((NC, len(OPS))),
        pltpu.SemaphoreType.DMA((NC, len(OPS))),
        pltpu.SemaphoreType.DMA((8, 16)),
        pltpu.SemaphoreType.DMA,
        pltpu.SemaphoreType.DMA((8, 16)),
    ]
    hbm = pl.BlockSpec(memory_space=pltpu.HBM)
    return pl.pallas_call(
        exchange,
        out_shape=jax.ShapeDtypeStruct(mat.shape, F32),
        in_specs=[hbm, hbm],
        out_specs=hbm,
        scratch_shapes=scratch,
        compiler_params=pltpu.CompilerParams(
            collective_id=0, has_side_effects=True, vmem_limit_bytes=67043328
        ),
        name="exchange",
    )(mat, refl)


def per_device(matrix, reflectors):
    refl = reflectors.reshape(2048, RANK)
    return project(matrix, refl)


def solution(mesh):
    placed = (P(None, "row", None, None, "col", None), P(None, "col", None, None))
    return jax.shard_map(
        per_device,
        mesh=mesh,
        in_specs=placed,
        out_specs=P(None, "row", None, None, "col", None),
        check_vma=False,
    )
```

time: 602 us -> 116 us (0.19); the launches traced: 593 us -> 116 us
  waiting for transfers between devices: 431 us -> 0 us
  Pallas kernels: 0 us -> 109 us
  matrix products: 89.6 us -> 0 us
  other arithmetic: 46.9 us -> 0 us
  between operations: 13.5 us -> 0.01 us
    psum x3 -> x0, waiting for transfers between devices: 342 us -> none  [the longest x2 240 us: from_root(): return lax.psum(kept, axis)]
    pallas_call x0 -> x1, Pallas kernels: none -> 109 us  [project(): pl.pallas_call(exchange, out_shape=jax.ShapeDtypeStruct(mat.shape, F32),...]
    dot_general x6 -> x0, matrix products: 89.6 us -> none  [the longest x1 33.6 us: per_device(): lax.dot_general(left_side, right_side, (((1,), (1,)), ((), ())), precisio...]
    reduce_scatter x1 -> x0, waiting for transfers between devices: 83.1 us -> none  [sum_by_parts(): lax.psum_scatter(rows_for(lines, lax.axis_size(axis)), axis, scatter_dime...]
    select_n x3 -> x0, other arithmetic: 38.6 us -> none  [the longest x1 32.2 us: per_device(): direct_part = matmul(jnp.where(lower_mask, current, 0.0), refl_cols)]
  transfers between devices with their start and end apart: 5 -> 0, of which waited for: 5 -> 0; matrix products, arithmetic and copies ran while one was open for 9% -> 0% of each run, Pallas kernels for 0% -> 0%
where the time goes in v1:
time: 116 us
  Pallas kernels  109 us (94%)
  local copies, waits for them, and re-layouts  6.96 us (6%)
    pallas_call x1, Pallas kernels, project(): pl.pallas_call(exchange, out_shape=jax.ShapeDtypeStruct(mat.shape, F32),...  109 us
    unnamed x1, local copies, waits for them, and re-layouts  6.96 us

profile of v1, /device:TPU:3, one launch (start us, length us, event | category | flops | bytes accessed | tf_op | source)
XLA Modules:
  0.0 116.3 jit_solution(7519107766462804173)
XLA Ops:
  0.0 109.4 %exchange.1 = f32[8,1,128,16,1,128]{5,4,3,2,1,0:T(1,128)} custom-call(f32[8,1,128,16,1,128]{5,4,3,2,1,0:T(1,128)} %mat.1, f32[2048,512]{1,0:T(8,128)} %bitcast.1), custom_call_target="tpu_custom_call" | custom-call | tf_op jit(solution)/shard_map/exchange/pallas_call | solution.py:505
  109.4 7.0 %copy.4 = f32[8,1,128,16,1,128]{5,4,3,2,1,0:T(1,128)} copy(f32[8,1,128,16,1,128]{5,4,3,2,1,0:T(1,128)} %exchange.1) | data formatting | bytes 16777216

commit v2 on v1

--- a/solution.py
+++ b/solution.py
@@ -10,16 +10,18 @@
 BF16 = jnp.bfloat16
 NC = 4
 PLAN = (
-    ("prep", (2, 0, 3)), ("dc", (3,)), ("v1", (0,)), ("dc", (2,)), ("v1", (1,)), ("prep", (1,)), ("v1", (2,)),
-    ("v2", (0,)), ("dc", (1, 0)), ("d1", (3,)), ("v2", (1,)), ("v1", (3,)), ("d1", (0,)), ("v3", (0, 1)),
-    ("v2", (2,)), ("vt", (0,)), ("d1", (1,)), ("v2", (3,)), ("vt", (1,)), ("v3", (2,)), ("t2", (0,)), ("v3", (3,)),
-    ("t2", (1,)), ("dx", (0,)), ("vt", (2,)), ("d1", (2,)), ("dx", (3, 1)), ("t3", (1, 0)), ("vt", (3,)),
-    ("t2", (2,)), ("t4", (1,)), ("d2", (1,)), ("t4", (0,)), ("d2", (0,)), ("dx", (2,)), ("t3", (2,)), ("d3", (1,)),
-    ("t5", (1,)), ("t2", (3,)), ("d3", (0,)), ("rz", (1,)), ("t4", (2,)), ("d2", (2,)), ("t5", (0,)), ("t3", (3,)),
-    ("cx", (1,)), ("t5", (2,)), ("rz", (0,)), ("d2", (3,)), ("d3", (2,)), ("t4", (3,)), ("a2", (1,)), ("rz", (2,)),
-    ("cx", (0,)), ("d3", (3,)), ("t5", (3,)), ("cx", (2,)), ("a3", (1,)), ("rz", (3,)), ("a2", (0,)), ("cx", (3,)),
-    ("a2", (2,)), ("a3", (0,)), ("a2", (3,)), ("a3", (2,)), ("a4", (0, 1)), ("a3", (3,)), ("a4", (2,)), ("a5", (0,)),
-    ("a4", (3,)), ("a5", (2, 1, 3)),
+    ("prep", (3, 2, 1)), ("dc", (2,)), ("v1", (0,)), ("dc", (1,)), ("v1", (1,)), ("prep", (0,)), ("dc", (0,)),
+    ("v1", (2,)), ("v2", (0,)), ("v1", (3,)), ("dc", (3,)), ("v2", (2,)), ("d1", (0, 2)), ("v3", (0, 2)),
+    ("v2", (3, 1)), ("vt", (0, 2)), ("d1", (3, 1)), ("t2", (0,)), ("v3", (3,)), ("dx", (0,)), ("t2", (2,)),
+    ("t3", (0,)), ("vt", (3,)), ("v3", (1,)), ("t3", (2,)), ("d2", (0,)), ("dx", (2, 3)), ("t2", (3,)), ("t4", (0,)),
+    ("d2", (2,)), ("t4", (2,)), ("d3", (0,)), ("vt", (1,)), ("t3", (3,)), ("t5", (0,)), ("d2", (3,)), ("t5", (2,)),
+    ("d3", (2,)), ("t2", (1,)), ("rz", (0,)), ("dx", (1,)), ("t4", (3,)), ("d3", (3,)), ("cb", (0,)), ("rz", (2,)),
+    ("t3", (1,)), ("d2", (1,)), ("ca", (0,)), ("t5", (3,)), ("cb", (2,)), ("t4", (1,)), ("ca", (2,)), ("rz", (3,)),
+    ("d3", (1,)), ("a2", (0,)), ("t5", (1,)), ("cb", (3,)), ("ca", (3,)), ("a2", (2,)), ("rz", (1,)), ("a3", (0,)),
+    ("b2", (0,)), ("cb", (1,)), ("ca", (1,)), ("b2", (2,)), ("a2", (3,)), ("a3", (2,)), ("b2", (3,)), ("a2", (1,)),
+    ("a4", (0,)), ("b3", (0, 2)), ("b2", (1,)), ("a4", (2,)), ("a5", (0,)), ("b3", (3,)), ("a3", (3, 1)),
+    ("a4", (3,)), ("b4", (0,)), ("b3", (1,)), ("a4", (1,)), ("a5", (3, 2)), ("b4", (1,)), ("a5", (1,)),
+    ("b4", (2, 3)),
 )
 RANK = 512
 W = RANK // NC
@@ -56,7 +58,7 @@
 def exchange(
     mat, refl, out,
     sbuf, sh, sl, vc, vcs, vr, vrs, vrt, dbuf, dh, dl, dr, d2r,
-    ubuf, t1r, t2r, t3r, crd, crt, rx, gbuf, wr, mm, wcts, wrs, zero,
+    ubuf, t1r, t2r, t3r, crd, crt, rx, gbuf, wr, mm, wcts, wrs,
     ssem, rsem, msem, vsem, osem,
 ):
     r, c = lax.axis_index("row"), lax.axis_index("col")
@@ -120,17 +122,9 @@
     for i in range(8):
         rows = pl.ds(i * 256, 256)
         vcs[0, rows, :], vcs[1, rows, :] = split(vc[rows, :])
-    zero[...] = jnp.zeros_like(zero)
-
-    def z_copy(i, kk, m):
-        return pltpu.make_async_copy(zero, out.at[2 * i + kk, 0, :, m, 0, :], osem.at[2 * i + kk, m])
-
-    def o_copy(i, kk, m):
-        return pltpu.make_async_copy(
-            sbuf.at[2 * i * (i + 1) + m, pl.ds(kk * 128, 128)],
-            out.at[2 * i + kk, 0, :, m, 0, :],
-            osem.at[2 * i + kk, m],
-        )
+    def o_copy(i, m):
+        spot = 2 * i * (i + 1) + m
+        return pltpu.make_async_copy(sbuf.at[spot], out.at[spot], osem.at[i, m])
 
     @pl.when(alone)
     def _():
@@ -158,7 +152,7 @@
 
     def v_copy(j):
         return send(
-            "V0", j, refl.at[pl.ds(pl.multiple_of(own * 128, 128), 128), pl.ds(j * W, W)],
+            "V0", j, vc.at[pl.ds(pl.multiple_of(own * 128, 128), 128), pl.ds(j * W, W)],
             vr.at[j, dz, dxl], to_d,
         )
 
@@ -185,11 +179,6 @@
             b = block(i, m // 4)
             cols = pl.ds((m % 4) * 128, 128)
             sh[b, :, cols], sl[b, :, cols] = split(x)
-
-        @pl.loop(4 * (i + 1), 16)
-        def _(m):
-            z_copy(i, 0, m).start()
-            z_copy(i, 1, m).start()
 
     def d_compute(i):
         acc = None
@@ -346,7 +335,7 @@
         for d in range(1, 4):
             start(f"R{d + 1}", j, rx.at[j, 1], rx.at[j, 1 + d], {"col": xl * 4 + rem(z + d, 4)})
 
-    def join(j):
+    def join_b(j):
         @pl.when(jnp.logical_not(alone))
         def _():
             got("CD", j, crd.at[j])
@@ -360,6 +349,8 @@
         wr[j, z, xl] = dbuf[j, xl, z] + crt[j].T
         start("B1", j, wr.at[j, z, xl], wr.at[j, z, xl], to_xl)
         gbuf[j, core, y, xh, 0:W, :] = ubuf[j, core, y, xh, 0:W, :] + crd[j].T
+
+    def join_a(j):
         total = rx[j, 1]
         for d in range(1, 4):
             got(f"R{d + 1}", j, rx.at[j, 1 + d])
@@ -367,19 +358,23 @@
         gbuf[j, core, y, xh, W:UW, :] = total
         start("A1", j, gbuf.at[j, core, y, xh], gbuf.at[j, core, y, xh], to_xh)
 
-    def a2(j):
+    def b2(j):
         got("B1", j, wr.at[j, z, 1 - xl])
         start("B2p", j, wr.at[j, z], wr.at[j, z], to_zp)
         start("B2m", j, wr.at[j, z], wr.at[j, z], to_zm)
+
+    def a2(j):
         got("A1", j, gbuf.at[j, core, y, 1 - xh])
         start("A2p", j, gbuf.at[j, core, y], gbuf.at[j, core, y], to_yp)
         start("A2m", j, gbuf.at[j, core, y], gbuf.at[j, core, y], to_ym)
 
-    def a3(j):
+    def b3(j):
         got("B2p", j, wr.at[j, zm])
         start("B3p", j, wr.at[j, zm, 0], wr.at[j, zm, 0], to_zp)
         got("B2m", j, wr.at[j, zp])
         start("B3m", j, wr.at[j, zp, 1], wr.at[j, zp, 1], to_zm)
+
+    def a3(j):
         got("A2p", j, gbuf.at[j, core, ym])
         start("A3p", j, gbuf.at[j, core, ym, 0], gbuf.at[j, core, ym, 0], to_yp)
         got("A2m", j, gbuf.at[j, core, yp])
@@ -389,6 +384,8 @@
         got("A3p", j, gbuf.at[j, core, y2, 0])
         got("A3m", j, gbuf.at[j, core, y2, 1])
         start("A4", j, gbuf.at[j, core], gbuf.at[j, core], to_core)
+
+    def b4(j):
         got("B3p", j, wr.at[j, z2, 0])
         got("B3m", j, wr.at[j, z2, 1])
 
@@ -411,7 +408,7 @@
     stages = {
         "prep": prep, "dc": d_compute, "v1": v1, "v2": v2, "v3": v3, "vt": v_ready,
         "d1": d1, "dx": dx, "d2": d2, "d3": d3, "t2": t2, "t3": t3, "t4": t4, "t5": t5, "rz": rz,
-        "cx": join, "a2": a2, "a3": a3, "a4": a4, "a5": a5,
+        "cb": join_b, "ca": join_a, "b2": b2, "b3": b3, "b4": b4, "a2": a2, "a3": a3, "a4": a4, "a5": a5,
     }
     for name, order in PLAN:
         for n in order:
@@ -442,8 +439,7 @@
                 if i == j:
                     x = jnp.where(diagonal(i) >= m * 1024, x, 0.0)
                 sbuf[2 * i * (i + 1) + m] = x
-                for kk in range(2):
-                    o_copy(i, kk, m).start()
+                o_copy(i, m).start()
     for copy in sent:
         copy.wait_send()
 
@@ -457,13 +453,52 @@
     for i in range(4):
         @pl.loop(0, 4 * (i + 1))
         def _(m):
-            o_copy(i, 0, m).wait()
-            o_copy(i, 1, m).wait()
-
-        @pl.loop(4 * (i + 1), 16)
-        def _(m):
-            z_copy(i, 0, m).wait()
-            z_copy(i, 1, m).wait()
+            o_copy(i, m).wait()
+
+
+def place(tiles, out, buf, zero, isem, osem):
+    def fetch(n):
+        return pltpu.make_async_copy(tiles.at[n], buf.at[n], isem.at[n])
+
+    def put(i, kk, m):
+        upper = m >= 4 * (i + 1)
+        src = zero if upper else buf.at[2 * i * (i + 1) + m, pl.ds(kk * 128, 128)]
+        return pltpu.make_async_copy(src, out.at[2 * i + kk, 0, :, m, 0, :], osem.at[2 * i + kk, m])
+
+    for n in range(40):
+        fetch(n).start()
+    zero[...] = jnp.zeros_like(zero)
+    every = [(i, m) for i in range(4) for m in range(16)]
+    for i, m in every:
+        if m >= 4 * (i + 1):
+            put(i, 0, m).start()
+            put(i, 1, m).start()
+    for i, m in every:
+        if m < 4 * (i + 1):
+            fetch(2 * i * (i + 1) + m).wait()
+            put(i, 0, m).start()
+            put(i, 1, m).start()
+    for i, m in every:
+        put(i, 0, m).wait()
+        put(i, 1, m).wait()
+
+
+def spread(tiles, shape):
+    hbm = pl.BlockSpec(memory_space=pltpu.HBM)
+    return pl.pallas_call(
+        place,
+        out_shape=jax.ShapeDtypeStruct(shape, F32),
+        in_specs=[hbm],
+        out_specs=hbm,
+        scratch_shapes=[
+            pltpu.VMEM((40, 256, 128), F32),
+            pltpu.VMEM((128, 128), F32),
+            pltpu.SemaphoreType.DMA((40,)),
+            pltpu.SemaphoreType.DMA((8, 16)),
+        ],
+        compiler_params=pltpu.CompilerParams(vmem_limit_bytes=67043328),
+        name="place",
+    )(tiles)
 
 
 def project(mat, refl):
@@ -494,17 +529,16 @@
         vm((RANK, RANK), F32),
         vm((2, RANK, 2048), BF16),
         vm((4, 2, 256, RANK), BF16),
-        vm((128, 128), F32),
         pltpu.SemaphoreType.DMA((NC, len(OPS))),
         pltpu.SemaphoreType.DMA((NC, len(OPS))),
         pltpu.SemaphoreType.DMA((8, 16)),
         pltpu.SemaphoreType.DMA,
-        pltpu.SemaphoreType.DMA((8, 16)),
+        pltpu.SemaphoreType.DMA((4, 16)),
     ]
     hbm = pl.BlockSpec(memory_space=pltpu.HBM)
     return pl.pallas_call(
         exchange,
-        out_shape=jax.ShapeDtypeStruct(mat.shape, F32),
+        out_shape=jax.ShapeDtypeStruct((40, 256, 128), F32),
         in_specs=[hbm, hbm],
         out_specs=hbm,
         scratch_shapes=scratch,
@@ -517,7 +551,7 @@
 
 def per_device(matrix, reflectors):
     refl = reflectors.reshape(2048, RANK)
-    return project(matrix, refl)
+    return spread(project(matrix, refl), matrix.shape)
 
 
 def solution(mesh):

time: 116 us -> 115 us (level)
  local copies, waits for them, and re-layouts: 6.96 us -> 0 us
  Pallas kernels: 109 us -> 114 us
    unnamed x1 -> x0, local copies, waits for them, and re-layouts: 6.96 us -> none
    pallas_call x1 -> x2, Pallas kernels: 109 us -> 114 us  [the longest x1 107 us: project(): pl.pallas_call(exchange, out_shape=jax.ShapeDtypeStruct((40, 256, 128), F...]
where the time goes in v2:
time: 115 us; the launch traced here: 114 us
  Pallas kernels  114 us (99%)
    pallas_call x1, Pallas kernels, project(): pl.pallas_call(exchange, out_shape=jax.ShapeDtypeStruct((40, 256, 128), F...  107 us
    pallas_call x1, Pallas kernels, spread(): pl.pallas_call(place, out_shape=jax.ShapeDtypeStruct(shape, F32), in_spec...  7.1 us

profile of v2, /device:TPU:3, one launch (start us, length us, event | category | flops | bytes accessed | tf_op | source)
XLA Modules:
  0.0 114.2 jit_solution(17696646098411211963)
XLA Ops:
  0.0 106.9 %exchange.1.tiles = f32[40,256,128]{2,1,0:T(8,128)} custom-call(f32[8,1,128,16,1,128]{5,4,3,2,1,0:T(1,128)} %mat.1, f32[2048,512]{1,0:T(8,128)} %bitcast.1), custom_call_target="tpu_custom_call" | custom-call | tf_op jit(solution)/shard_map/exchange/pallas_call | solution.py:539
  106.9 7.1 %place.1 = f32[8,1,128,16,1,128]{5,4,3,2,1,0:T(1,128)} custom-call(f32[40,256,128]{2,1,0:T(8,128)} %exchange.1.tiles), custom_call_target="tpu_custom_call" | custom-call | tf_op jit(solution)/shard_map/place/pallas_call | solution.py:488
